TPU v7x, 32 devices: a whole 2x2x4 slice. The times are simulated.
32 devices in a mesh: tm: 8 (over z, x), tp: 4 (over y, core).
Axes of the slice: x: 2, y: 2, z: 4, core: 2. Of those that a mesh axis runs over, the one named last changes fastest.
Arguments:
- trajectory: float32 [16, 128, 3072], P('tm', None, 'tp'), may hold values from -6 to 6
- offset: int32 [1], replicated, may hold values from 0 to 15
- step_gaps: int32 [16], P('tm'), may hold values from 1 to 4, as said below
- qkv_weight: bfloat16 [3072, 3, 3072], P(None, None, 'tp')
- out_weight: bfloat16 [3072, 3072], P('tp'), may hold values from -4 to 4
- mod_weight: bfloat16 [256, 3, 3072], P(None, None, 'tp'), may hold values from -0.375 to 0.375
Outputs:
- advanced: float32 [16, 128, 3072], P('tm', None, 'tp')
Inputs may be any that keep to these rules, and one draw needn't show every extreme that they name: `step_gaps`: in aligned blocks of 2 timesteps, the gaps of block b sum to an even number for even b and to an odd number for odd b.
All inputs are finite; a program needn't handle non-finite values.
Results may differ from a plain program's by a relative error of at most 0.007.
Values may be sent and summed in bfloat16 or wider, within the bound.
A program may use at most 128 MiB of HBM per device.

v0:
```python
import math

import jax
import jax.numpy as jnp
from jax import lax
from jax.sharding import PartitionSpec as P

HD = 128
FREQ = 256
ITERS = 2


def prefix(array, axis, combine, identity):
    size, place = (lax.axis_size(axis), lax.axis_index(axis))
    everything = lax.all_gather(array, axis)
    start = jnp.broadcast_to(jnp.asarray(identity, array.dtype), array.shape)

    def turn(k, before):
        reached = k < place
        new = combine(before, everything[k])
        return jnp.where(reached, new, before)

    return lax.fori_loop(0, size, turn, start)


def prefix_2(array, axis, join, neutral):
    place = lax.axis_index(axis)
    gathered = lax.all_gather(array.astype(jnp.bfloat16), axis)
    state = jnp.zeros_like(array) + jnp.asarray(neutral, array.dtype)

    def one(turn, state):
        return join(state, lax.dynamic_index_in_dim(gathered, turn, 0, False).astype(array.dtype))

    return lax.fori_loop(0, place, one, state)


def add_up(earlier, later):
    return earlier + later


def embedding(sigma):
    half_freq = FREQ // 2
    frequencies = jnp.exp(-math.log(10000.0) * jnp.arange(half_freq, dtype=jnp.float32) / half_freq)
    angles = 1000.0 * sigma[:, None] * frequencies[None, :]
    return jnp.concatenate([jnp.cos(angles), jnp.sin(angles)], -1).astype(jnp.bfloat16)


def body(trajectory, offset, step_gaps, qkv_weight, out_weight, mod_weight):
    steps_here, tok_count, col_count = trajectory.shape
    full_width = qkv_weight.shape[0]
    time_count = steps_here * lax.axis_size("tm")
    level_count = 5 * time_count
    before = prefix(jnp.sum(step_gaps), "tm", add_up, jnp.int32(0))
    levels = (offset[0] + before + jnp.cumsum(step_gaps) - step_gaps).astype(jnp.float32)
    sigma = 1.0 - levels / level_count
    step_size = step_gaps.astype(jnp.float32) / level_count
    embed_rows = embedding(sigma)
    full_mod = lax.all_gather(mod_weight, "tp", axis=2, tiled=True)
    modulation = jnp.dot(
        embed_rows, full_mod.reshape(FREQ, 3 * full_width), preferred_element_type=jnp.float32
    ).reshape(steps_here, 3, full_width)
    gate_rows = lax.dynamic_slice_in_dim(
        modulation[:, 2], lax.axis_index("tp") * col_count, col_count, 1
    )
    first_point = jnp.where(lax.axis_index("tm") == 0, trajectory[0], jnp.zeros_like(trajectory[0]))
    flat_qkv = qkv_weight.reshape(full_width, -1)
    states = trajectory
    points = trajectory
    for sweep in range(ITERS):
        whole_rows = lax.all_gather(states, "tp", axis=2, tiled=True)
        row_mean = jnp.sum(whole_rows, -1, keepdims=True) / full_width
        variance = (
            jnp.sum(whole_rows * whole_rows, -1, keepdims=True) / full_width - row_mean * row_mean
        )
        inv_std = lax.rsqrt(variance + 1e-06)
        normed = (
            (whole_rows - row_mean) * inv_std * (1.0 + modulation[:, 1][:, None, :])
            + modulation[:, 0][:, None, :]
        ).astype(jnp.bfloat16)
        projected = jnp.einsum("std,de->ste", normed, flat_qkv, preferred_element_type=jnp.float32)
        projected = projected.astype(jnp.bfloat16).reshape(steps_here, tok_count, 3, -1, HD)
        queries = projected[:, :, 0]
        key_rows = projected[:, :, 1]
        values = projected[:, :, 2]
        scores = jnp.einsum(
            "sqhd,skhd->shqk", queries, key_rows, preferred_element_type=jnp.float32
        ) * (1.0 / math.sqrt(HD))
        row_max = jnp.max(scores, -1, keepdims=True)
        weights_exp = jnp.exp(scores - row_max)
        probs = (weights_exp / jnp.sum(weights_exp, -1, keepdims=True)).astype(jnp.bfloat16)
        attended = jnp.einsum(
            "shqk,skhd->sqhd", probs, values, preferred_element_type=jnp.float32
        ).astype(jnp.bfloat16)
        attended = attended.reshape(steps_here, tok_count, -1)
        head_out = jnp.einsum(
            "sqe,ed->sqd", attended, out_weight, preferred_element_type=jnp.float32
        )
        col_share = lax.psum_scatter(
            head_out.astype(jnp.bfloat16), "tp", scatter_dimension=2, tiled=True
        ).astype(jnp.float32)
        drifts = gate_rows[:, None, :] * col_share
        increments = -step_size[:, None, None] * drifts
        local_cum = jnp.cumsum(increments, 0)
        prefix_sum = prefix_2(
            local_cum[-1] + first_point,
            "tm",
            add_up,
            jnp.zeros((tok_count, col_count), jnp.float32),
        )
        entry_point = prefix_sum + first_point
        points = entry_point[None] + local_cum
        states = jnp.concatenate([entry_point[None], points[:-1]], 0)
    return points


def solution(mesh):
    placed = (
        P("tm", None, "tp"),
        P(),
        P("tm"),
        P(None, None, "tp"),
        P("tp", None),
        P(None, None, "tp"),
    )
    return jax.shard_map(
        body, mesh=mesh, in_specs=placed, out_specs=P("tm", None, "tp"), check_vma=False
    )
```

profile of v0, /device:TPU:24, one launch (start us, length us, event | category | flops | bytes accessed | tf_op | source)
XLA Modules:
  0.0 313.6 jit_solution(12103827058173000939)
XLA Ops:
  7.3 2.4 copy.33
  11.1 1.4 dynamic-update-slice
  12.6 7.7 %all-reduce = s32[8]{0:T(128)S(1)} all-reduce(s32[8]{0:T(128)S(1)} %dynamic-update-slice), channel_id=1, replica_groups=mesh['tm'=8,'tp'=4] {'tm'}, use_global_device_ids=true, to_apply=%add | all-reduce | flops 8 | bytes 64
  21.1 18.7 %copy.34 = bf16[3072,3,768]{0,2,1:T(8,128)(2,1)} copy(bf16[3072,3,768]{2,0,1:T(8,128)(2,1)} %param.15) | data formatting | bytes 28311552 | tf_op args[3]
  39.8 10.1 %while.33 = (s32[]{:T(128)}, s32[]{:T(128)}, s32[]{:T(128)}, s32[8]{0:T(128)S(1)}, s32[]{:T(128)}) while((s32[]{:T(128)}, s32[]{:T(128)}, s32[]{:T(128)}, s32[8]{0:T(128)S(1)}, s32[]{:T(128)}) %tuple.62), condition=%wide.region_2.3_spmd, body=%wide.region_1.2_spmd.sunk | while | flops 5 | bytes 107 | solution.py:23
  50.1 2.5 fusion.57
  52.6 24.8 %all-gather.6.cloned.1.call-done = bf16[256,3,3072]{0,2,1:T(8,128)(2,1)} async-done(((bf16[256,3,768]{0,2,1:T(8,128)(2,1)}), bf16[256,3,3072]{0,2,1:T(8,128)(2,1)}) %all-gather.6.cloned.1.call-update) | async-done | bytes 4718608 | tf_op jit(solution)/shard_map/all_gather | solution.py:58
  77.4 3.6 %fusion.2 = f32[2,3,3072]{2,0,1:T(2,128)S(1)} fusion(bf16[256,3,3072]{0,2,1:T(8,128)(2,1)} %all-gather.6.cloned.1.call-done, bf16[2,128]{1,0:T(2,128)(2,1)S(1)} %get-tuple-element.169, bf16[2,128]{1,0:T(2,128)(2,1)S(1)} %get-tuple-element.168), kind=kOutput, calls=%fused_computation.4 | convolution fusion | flops 9439232 | bytes 4793344 | tf_op jit(solution)/shard_map/dot_general | solution.py:59
  81.1 10.0 %convolution_convert_fusion.1 = bf16[2,128,2304]{2,1,0:T(8,128)(2,1)S(1)} fusion(bf16[3072,2304,1]{0,1,2:T(8,128)(2,1)} %bitcast.117, f32[2,128,3072]{2,1,0:T(8,128)} %all-gather.8.cloned.1.call-done, f32[2,3072]{1,0:T(2,128)S(1)} %get-tuple-element.162, f32[2,3072]{1,0:T(2,128)S(1)} %get-tuple-element.163, f32[2,128]{1,0:T(2,128)S(1)} %get-tuple-element.167, ...), kind=kOutput, calls=%fused_computation.13 | convolution fusion | flops 3628400640 | bytes 18532352 | tf_op jit(solution)/shard_map/std,de->ste/dot_general | solution.py:80
  93.0 5.0 %fusion.8 = bf16[2,128,3072]{2,1,0:T(8,128)(2,1)} fusion(bf16[2,128,768]{1,2,0:T(8,128)(2,1)S(1)} %bitcast.126, bf16[768,3072]{1,0:T(8,128)(2,1)} %param.16), kind=kOutput, calls=%fused_computation.10 | convolution fusion | flops 1208745984 | bytes 6684672 | tf_op jit(solution)/shard_map/sqe,ed->sqd/dot_general | solution.py:95
  98.1 28.2 %reduce-scatter.3.cloned.1.call-done = bf16[2,128,768]{2,1,0:T(8,128)(2,1)} async-done(((bf16[2,128,3072]{2,1,0:T(8,128)(2,1)}), bf16[2,128,768]{2,1,0:T(8,128)(2,1)}) %reduce-scatter.3.cloned.1.call-update) | async-done | bytes 393232 | tf_op jit(solution)/shard_map/reduce_scatter | solution.py:98
  126.3 1.1 fusion.30
  128.2 42.7 %all-gather.10.cloned.1.call-done = bf16[8,128,768]{2,1,0:T(8,128)(2,1)} async-done(((bf16[1,128,768]{2,1,0:T(8,128)(2,1)}), bf16[8,128,768]{2,1,0:T(8,128)(2,1)}) %all-gather.10.cloned.1.call-update) | async-done | bytes 1572880 | tf_op jit(solution)/shard_map/all_gather | solution.py:28
  170.9 6.2 %while.34 = (s32[]{:T(128)}, f32[128,768]{1,0:T(8,128)S(1)}, s32[]{:T(128)}, bf16[8,128,768]{2,1,0:T(8,128)(2,1)}, s32[]{:T(128)}, /*index=5*/s32[]{:T(128)}, s32[]{:T(128)}) while((s32[]{:T(128)}, f32[128,768]{1,0:T(8,128)S(1)}, s32[]{:T(128)}, bf16[8,128,768]{2,1,0:T(8,128)(2,1)}, s32[]{:T(128)}, /*index=5*/s32[]{:T(128)}, ...), condition=%wide.region_11.12_spmd, body=%wide.region_10.11_spmd.sunk | while | flops 196613 | bytes 983155 | solution.py:34
  170.9 1.0 convert_add_fusion.4
  171.9 1.0 convert_add_fusion.4
  178.4 29.5 %all-gather.12.cloned.1.call-done = f32[2,128,3072]{2,1,0:T(8,128)} async-done(((f32[2,128,768]{2,1,0:T(8,128)}), f32[2,128,3072]{2,1,0:T(8,128)}) %all-gather.12.cloned.1.call-update) | async-done | bytes 3145744 | tf_op jit(solution)/shard_map/all_gather | solution.py:70
  207.8 2.6 fusion.56
  210.7 9.2 %convolution_convert_fusion = bf16[2,128,2304]{2,1,0:T(8,128)(2,1)S(1)} fusion(bf16[3072,2304,1]{0,1,2:T(8,128)(2,1)} %bitcast.118, f32[2,128,3072]{2,1,0:T(8,128)S(1)} %copy-done.1, f32[2,128]{1,0:T(2,128)S(1)} %get-tuple-element.165, f32[2,128]{1,0:T(2,128)S(1)} %get-tuple-element.164, f32[2,3072]{1,0:T(2,128)} %copy-done.2, f32[2,3072]{1,0:T(2,128)} %copy-done.3), kind=kOutput, calls=%fused_computation.12 | convolution fusion | flops 3628400640 | bytes 18532352 | tf_op jit(solution)/shard_map/std,de->ste/dot_general | solution.py:80
  221.7 4.9 %fusion.11 = bf16[2,128,3072]{2,1,0:T(8,128)(2,1)} fusion(bf16[2,128,768]{1,2,0:T(8,128)(2,1)S(1)} %bitcast.127, bf16[768,3072]{1,0:T(8,128)(2,1)} %param.16), kind=kOutput, calls=%fused_computation.11 | convolution fusion | flops 1208745984 | bytes 6684672 | tf_op jit(solution)/shard_map/sqe,ed->sqd/dot_general | solution.py:95
  226.7 28.1 %reduce-scatter.5.cloned.1.call-done = bf16[2,128,768]{2,1,0:T(8,128)(2,1)} async-done(((bf16[2,128,3072]{2,1,0:T(8,128)(2,1)}), bf16[2,128,768]{2,1,0:T(8,128)(2,1)}) %reduce-scatter.5.cloned.1.call-update) | async-done | bytes 393232 | tf_op jit(solution)/shard_map/reduce_scatter | solution.py:98
  254.8 1.1 fusion.26
  256.7 42.9 %all-gather.14.cloned.1.call-done = bf16[8,128,768]{2,1,0:T(8,128)(2,1)} async-done(((bf16[1,128,768]{2,1,0:T(8,128)(2,1)}), bf16[8,128,768]{2,1,0:T(8,128)(2,1)}) %all-gather.14.cloned.1.call-update) | async-done | bytes 1572880 | tf_op jit(solution)/shard_map/all_gather | solution.py:28
  299.6 6.2 %while.35 = (s32[]{:T(128)}, f32[128,768]{1,0:T(8,128)S(1)}, s32[]{:T(128)}, bf16[8,128,768]{2,1,0:T(8,128)(2,1)}, s32[]{:T(128)}, /*index=5*/s32[]{:T(128)}, s32[]{:T(128)}) while((s32[]{:T(128)}, f32[128,768]{1,0:T(8,128)S(1)}, s32[]{:T(128)}, bf16[8,128,768]{2,1,0:T(8,128)(2,1)}, s32[]{:T(128)}, /*index=5*/s32[]{:T(128)}, ...), condition=%wide.region_19.20_spmd, body=%wide.region_18.19_spmd.sunk | while | flops 196613 | bytes 983155 | solution.py:34
  (73 shorter events, 25.2 us)
Async XLA Ops:
  6.5 3.3 %copy-start.5 = (u32[32]{0:T(128)S(1)}, u32[32]{0:T(128)}, u32[]{:S(2)}) copy-start(u32[32]{0:T(128)} %constant.91) | copy-start | bytes 388
  6.5 3.9 %copy-start.4 = (s32[2]{0:T(128)S(1)}, s32[2]{0:T(128)}, u32[]{:S(2)}) copy-start(s32[2]{0:T(128)} %param.14) | copy-start | bytes 28
  6.5 43.5 %all-gather.8.cloned.1.call-start = ((), (), s32[]{:S(2)}) async-start(), calls=%async_computation.3 | async-start | bytes 3932160 | tf_op jit(solution)/shard_map/all_gather | solution.py:70
  7.3 70.2 %all-gather.6.cloned.1.call-start = ((), (), s32[]{:S(2)}) async-start(), calls=%async_computation.2 | async-start | bytes 5898240 | tf_op jit(solution)/shard_map/all_gather | solution.py:58
  9.7 116.5 %reduce-scatter.3.cloned.1.call-start = ((), (), s32[]{:S(2)}) async-start(), calls=%async_computation.4 | async-start | bytes 1966080 | tf_op jit(solution)/shard_map/reduce_scatter | solution.py:98
  81.1 10.0 %copy-start.2 = (f32[2,3072]{1,0:T(2,128)}, f32[2,3072]{1,0:T(2,128)S(1)}, u32[]{:S(2)}) copy-start(f32[2,3072]{1,0:T(2,128)S(1)} %get-tuple-element.162) | copy-start | bytes 73732
  81.1 10.0 %copy-start.3 = (f32[2,3072]{1,0:T(2,128)}, f32[2,3072]{1,0:T(2,128)S(1)}, u32[]{:S(2)}) copy-start(f32[2,3072]{1,0:T(2,128)S(1)} %get-tuple-element.163) | copy-start | bytes 73732
  93.0 34.4 %copy-start = (f32[2,128,768]{2,1,0:T(8,128)S(1)}, f32[2,128,768]{2,1,0:T(8,128)}, u32[]{:S(2)}) copy-start(f32[2,128,768]{2,1,0:T(8,128)} %param.12) | copy-start | bytes 2359300
  98.0 72.8 %all-gather.10.cloned.1.call-start = ((), (), s32[]{:S(2)}) async-start(), calls=%async_computation.5 | async-start | bytes 1769472 | tf_op jit(solution)/shard_map/all_gather | solution.py:28
  128.1 79.7 %all-gather.12.cloned.1.call-start = ((), (), s32[]{:S(2)}) async-start(), calls=%async_computation.6 | async-start | bytes 3932160 | tf_op jit(solution)/shard_map/all_gather | solution.py:70
  178.1 76.7 %reduce-scatter.5.cloned.1.call-start = ((), (), s32[]{:S(2)}) async-start(), calls=%async_computation.7 | async-start | bytes 1966080 | tf_op jit(solution)/shard_map/reduce_scatter | solution.py:98
  207.8 2.8 copy-start.1
  226.6 72.9 %all-gather.14.cloned.1.call-start = ((), (), s32[]{:S(2)}) async-start(), calls=%async_computation.8 | async-start | bytes 1769472 | tf_op jit(solution)/shard_map/all_gather | solution.py:28
Sparse Core Ops, SparseCore 0:
  8.9 29.4 all-gather.7
  40.0 37.4 all-gather.5
  98.2 28.0 reduce-scatter.2
  128.3 42.4 all-gather.9
  178.2 29.5 all-gather.11
  226.7 28.0 reduce-scatter.4
  257.0 42.5 all-gather.13
where the time goes:
time: 315 us; the launch traced here: 314 us
  waiting for transfers between devices  197 us (63%)
  matrix products  34.9 us (11%)
  local copies, waits for them, and re-layouts  29.8 us (9%)
  other arithmetic  23.8 us (8%)
  between operations  14.4 us (5%)
  blocking collectives  7.72 us (2%)
  loops' own time  5.61 us (2%)
    all_gather x2, waiting for transfers between devices, prefix_2(): gathered = lax.all_gather(array.astype(jnp.bfloat16), axis)  85.5 us
    reduce_scatter x2, waiting for transfers between devices, body(): lax.psum_scatter(head_out.astype(jnp.bfloat16), 'tp', scatter_dimension=2...  56.3 us
    all_gather x2, waiting for transfers between devices, body(): whole_rows = lax.all_gather(states, 'tp', axis=2, tiled=True)  29.5 us
    all_gather x1, waiting for transfers between devices, body(): full_mod = lax.all_gather(mod_weight, 'tp', axis=2, tiled=True)  24.8 us
    unnamed x17, local copies, waits for them, and re-layouts  23.4 us
    dot_general x2, matrix products, body(): jnp.einsum('std,de->ste', normed, flat_qkv, preferred_element_type=jnp.fl...  19.1 us
    add x12, other arithmetic, add_up(): return earlier + later  12 us
    dot_general x2, matrix products, body(): jnp.einsum('sqe,ed->sqd', attended, out_weight, preferred_element_type=jn...  9.87 us
  transfers between devices with their start and end apart: 7, of which 6 were waited for; matrix products, arithmetic and copies ran while one was open for 10% of the time, Pallas kernels for 0%

commit v1 on v0

v1 whole, which is shorter than its diff:
```python
import functools
import math

import jax
import jax.numpy as jnp
from jax import lax
from jax.experimental import pallas as pl
from jax.experimental.pallas import tpu as pltpu
from jax.sharding import PartitionSpec as P

HD = 128
FREQ = 256
ITERS = 2
F32 = jnp.float32
BF16 = jnp.bfloat16
MESH = pl.DeviceIdType.MESH


def level_table(level_count):
    rows = -(-level_count // 128) * 128
    sigma = 1.0 - jnp.arange(rows, dtype=jnp.int32).astype(F32) / level_count
    half_freq = FREQ // 2
    frequencies = jnp.exp(-math.log(10000.0) * jnp.arange(half_freq, dtype=F32) / half_freq)
    angles = 1000.0 * sigma[:, None] * frequencies[None, :]
    return jnp.concatenate([jnp.cos(angles), jnp.sin(angles)], -1).astype(BF16)


def kernel(
    tm, tp, steps, tok, col,
    offset, gaps, traj_hbm, table_hbm, mod_hbm, qkv_hbm, out_hbm, result,
    traj, table, mod_w, qkv_w, out_w, mods,
    gap_buf, stat_buf, normed, acc, attended,
    rs_part, rs_cross, inc, tot, pair_send, pair_recv, chain_send, chain_recv,
    last_send, last_recv, prefix, start, start_b,
    load_sem, gap_send_sem, gap_recv_sem, stat_sem, ag_sem, rs_sem, scan_sem,
    chain_sem, start_send_sem, start_recv_sem,
):
    k = lax.axis_index("tm")
    j = lax.axis_index("tp")
    rows = steps * tok
    width = tp * col
    half = col // 2
    groups = tp // 2
    pairs = tm // 2
    core = lax.rem(j, 2)
    group = lax.div(j, 2)
    side = lax.rem(k, 2)
    link = lax.div(k, 2)
    partner = group * 2 + (1 - core)
    neighbour = link * 2 + (1 - side)

    loads = [
        pltpu.make_async_copy(src, dst, load_sem.at[n])
        for n, (src, dst) in enumerate(
            ((traj_hbm, traj), (table_hbm, table), (mod_hbm, mod_w), (qkv_hbm, qkv_w), (out_hbm, out_w))
        )
    ]
    for load in loads:
        load.start()

    barrier = pltpu.get_barrier_semaphore()
    for d in range(1, tp):
        pl.semaphore_signal(
            barrier, inc=1, device_id=(k, lax.rem(j + d, tp)), device_id_type=MESH
        )
    for d in range(1, tm):
        pl.semaphore_signal(
            barrier, inc=1, device_id=(lax.rem(k + d, tm), j), device_id_type=MESH
        )

    def send(src, dst, send_sem, recv_sem, to_k, to_j):
        return pltpu.make_async_remote_copy(
            src_ref=src, dst_ref=dst, send_sem=send_sem, recv_sem=recv_sem,
            device_id=(to_k, to_j), device_id_type=MESH,
        )

    own_total = gaps[0]
    for s in range(1, steps):
        own_total = own_total + gaps[s]
    gap_buf[0] = jnp.full((8, 128), own_total, jnp.int32)
    loads[0].wait()

    def stats_of(sweep):
        x = traj[...].reshape(rows, col)
        total = jnp.sum(x, -1, keepdims=True)
        squares = jnp.sum(x * x, -1, keepdims=True)
        lane = lax.broadcasted_iota(jnp.int32, (rows, 128), 1)
        both = jnp.where(lane == 0, total, jnp.where(lane == 1, squares, 0.0))
        stat_buf[sweep, 0] = jnp.transpose(both)[0:8]

    stats_of(0)
    start_b[0] = traj[0].astype(BF16)
    pl.semaphore_wait(barrier, tp - 1 + tm - 1)

    def stat_copy(sweep, d):
        return send(
            stat_buf.at[sweep, 0], stat_buf.at[sweep, d],
            stat_sem.at[sweep, 0, d], stat_sem.at[sweep, 1, d], k, lax.rem(j + d, tp),
        )

    def gap_copy(d):
        return send(
            gap_buf.at[0], gap_buf.at[d], gap_send_sem.at[d], gap_recv_sem.at[d],
            lax.rem(k + d, tm), j,
        )

    def start_copy(d):
        return send(start_b.at[0], start_b.at[1], start_send_sem.at[d], start_recv_sem, d, j)

    for d in range(1, tm):
        gap_copy(d).start()
    for d in range(1, tp):
        stat_copy(0, d).start()

    @pl.when(k == 0)
    def _():
        for d in range(1, tm):
            start_copy(d).start()

    before = jnp.full((8, 128), offset[0], jnp.int32)
    for d in range(1, tm):
        gap_copy(d).wait_recv()
        before = before + jnp.where(k >= d, gap_buf[d], 0)
    row = lax.broadcasted_iota(jnp.int32, (8, 128), 0)
    for s in range(steps):
        before = before + jnp.where(row > s, gaps[s], 0)
    loads[1].wait()
    table_rows = table.shape[0]
    levels = jnp.concatenate([before] * (table_rows // 128), -1)
    pick = (lax.broadcasted_iota(jnp.int32, (8, table_rows), 1) == levels).astype(F32).astype(BF16)
    embed = jnp.dot(pick, table[...], preferred_element_type=F32).astype(BF16)
    loads[2].wait()
    for part in range(3):
        mods[part] = jnp.dot(embed, mod_w[part], preferred_element_type=F32)

    def ag_copy(sweep, kind, g, s):
        sems = (ag_sem.at[sweep, 0, kind, g, s], ag_sem.at[sweep, 1, kind, g, s])
        if kind == 0:
            return send(normed.at[sweep, 0, s], normed.at[sweep, 1, s], *sems, k, partner)
        if kind == 1:
            there = lax.rem(group + g, groups) * 2 + core
            return send(normed.at[sweep, 0, s], normed.at[sweep, 2 * g, s], *sems, k, there)
        return send(normed.at[sweep, 2 * g, s], normed.at[sweep, 2 * g + 1, s], *sems, k, partner)

    def part_copy(sweep, g):
        return send(
            rs_part.at[sweep, 0, g], rs_part.at[sweep, 1, g],
            rs_sem.at[sweep, 0, 0, g], rs_sem.at[sweep, 1, 0, g], k, partner,
        )

    def cross_copy(sweep, g):
        there = lax.rem(group + g, groups) * 2 + core
        return send(
            rs_cross.at[sweep, 0, g - 1], rs_cross.at[sweep, 1, g - 1],
            rs_sem.at[sweep, 0, 1, g], rs_sem.at[sweep, 1, 1, g], k, there,
        )

    def pair_copy(sweep):
        return send(
            pair_send.at[sweep], pair_recv.at[sweep],
            scan_sem.at[sweep, 0, 0], scan_sem.at[sweep, 1, 0], neighbour, j,
        )

    def last_copy(sweep, c):
        return send(
            last_send.at[sweep, c], last_recv.at[sweep, c],
            chain_sem.at[sweep, 2, c], chain_sem.at[sweep, 3, c], neighbour, j,
        )

    def chain_copy(sweep, c):
        return send(
            chain_send.at[sweep, c], chain_recv.at[sweep, c],
            chain_sem.at[sweep, 0, c], chain_sem.at[sweep, 1, c], lax.rem(k + 2, tm), j,
        )

    chunks = chain_send.shape[1]
    piece = tok // chunks

    for sweep in range(ITERS):
        if sweep > 0:
            stats_of(sweep)
            for d in range(1, tp):
                stat_copy(sweep, d).start()
        stats = stat_buf[sweep, 0]
        for d in range(1, tp):
            stat_copy(sweep, d).wait_recv()
            stats = stats + stat_buf[sweep, d]
        stats = jnp.transpose(
            jnp.concatenate([stats, jnp.zeros((120, rows), F32)], 0)
        )
        row_mean = stats[:, 0:1] / width
        variance = stats[:, 1:2] / width - row_mean * row_mean
        inv_std = lax.rsqrt(variance + 1e-06)
        for s in range(steps):
            part = slice(s * tok, (s + 1) * tok)
            normed[sweep, 0, s] = (
                (traj[s] - row_mean[part]) * inv_std[part] * (1.0 + mods[1, s : s + 1])
                + mods[0, s : s + 1]
            ).astype(BF16)
            for g in range(1, groups):
                ag_copy(sweep, 1, g, s).start()
            ag_copy(sweep, 0, 0, s).start()

        if sweep == 0:
            loads[3].wait()

        def project(slot, owner):
            block = normed[sweep, slot].reshape(rows, col)
            at = pl.multiple_of(owner * col, col)

            def one(part, carry):
                product = jnp.dot(block, qkv_w[part, pl.ds(at, col), :], preferred_element_type=F32)
                if slot == 0:
                    acc[part] = product
                else:
                    acc[part] = acc[part] + product
                return carry

            lax.fori_loop(0, 3, one, 0)

        project(0, j)
        for s in range(steps):
            ag_copy(sweep, 0, 0, s).wait_recv()
        project(1, partner)
        for g in range(1, groups):
            for s in range(steps):
                ag_copy(sweep, 1, g, s).wait_recv()
                ag_copy(sweep, 2, g, s).start()
            owner = lax.rem(group + groups - g, groups) * 2
            project(2 * g, owner + core)
            for s in range(steps):
                ag_copy(sweep, 2, g, s).wait_recv()
            project(2 * g + 1, owner + 1 - core)

        def attend(s, carry):
            at = pl.ds(pl.multiple_of(s * tok, tok), tok)
            for head in range(col // HD):
                lanes = slice(head * HD, (head + 1) * HD)
                queries = acc[0, at, lanes].astype(BF16)
                key_rows = acc[1, at, lanes].astype(BF16)
                values = acc[2, at, lanes].astype(BF16)
                scores = lax.dot_general(
                    queries, key_rows, (((1,), (1,)), ((), ())), preferred_element_type=F32
                ) * (1.0 / math.sqrt(HD))
                weights_exp = jnp.exp(scores - jnp.max(scores, -1, keepdims=True))
                probs = (weights_exp / jnp.sum(weights_exp, -1, keepdims=True)).astype(BF16)
                attended[at, lanes] = jnp.dot(
                    probs, values, preferred_element_type=F32
                ).astype(BF16)
            return carry

        lax.fori_loop(0, steps, attend, 0)
        if sweep == 0:
            loads[4].wait()

        def head_out(dest):
            at = pl.ds(pl.multiple_of(dest * col, col), col)
            return jnp.dot(attended[...], out_w[:, at], preferred_element_type=F32)

        for g in list(range(1, groups)) + [0]:
            there = lax.rem(group + g, groups) * 2
            rs_part[sweep, 0, g] = head_out(there + 1 - core).astype(BF16)
            part_copy(sweep, g).start()
            mine = head_out(there + core)
            if g > 0:
                part_copy(sweep, g).wait_recv()
                rs_cross[sweep, 0, g - 1] = (mine + rs_part[sweep, 1, g].astype(F32)).astype(BF16)
                cross_copy(sweep, g).start()
            else:
                inc[...] = mine.reshape(steps, tok, col)
        part_copy(sweep, 0).wait_recv()
        share = inc[...].reshape(rows, col) + rs_part[sweep, 1, 0].astype(F32)
        for g in range(1, groups):
            cross_copy(sweep, g).wait_recv()
            share = share + rs_cross[sweep, 1, g - 1].astype(F32)

        running = jnp.zeros((tok, col), F32)
        for s in range(steps):
            size = gaps[s].astype(F32) / (5 * steps * tm)
            running = running - size * (mods[2, s : s + 1] * share[s * tok : (s + 1) * tok])
            inc[s] = running
        for h in range(2):
            tot[h] = running[:, h * half : (h + 1) * half]
        pair_send[sweep] = tot[1 - side].astype(BF16)
        pair_copy(sweep).start()

        @pl.when(link == 0)
        def _():
            chain_recv[sweep] = jnp.zeros_like(chain_recv[sweep])

        pair_copy(sweep).wait_recv()
        first = side == 0
        for c in range(chunks):
            at = slice(c * piece, (c + 1) * piece)
            ours = tot[side, at]
            theirs = pair_recv[sweep, at].astype(F32)

            @pl.when(link > 0)
            def _():
                chain_copy(sweep, c).wait_recv()

            earlier = chain_recv[sweep, c].astype(F32)

            @pl.when(link < pairs - 1)
            def _():
                chain_send[sweep, c] = (earlier + ours + theirs).astype(BF16)
                chain_copy(sweep, c).start()

            last_send[sweep, c] = jnp.where(first, earlier + ours, earlier).astype(BF16)
            last_copy(sweep, c).start()
            prefix[side, at] = jnp.where(first, earlier, earlier + theirs)
        if sweep == 0:
            @pl.when(k > 0)
            def _():
                start_copy(1).wait_recv()
                start[...] = start_b[1].astype(F32)

            @pl.when(k == 0)
            def _():
                start[...] = traj[0]
        for c in range(chunks):
            last_copy(sweep, c).wait_recv()
            prefix[1 - side, c * piece : (c + 1) * piece] = last_recv[sweep, c].astype(F32)
        entry = start[...] + jnp.concatenate([prefix[0], prefix[1]], -1)
        if sweep < ITERS - 1:
            traj[0] = entry
            for s in range(1, steps):
                traj[s] = entry + inc[s - 1]
        else:
            for s in range(steps):
                result[s] = entry + inc[s]

    for d in range(1, tm):
        gap_copy(d).wait_send()

    @pl.when(k == 0)
    def _():
        for d in range(1, tm):
            start_copy(d).wait_send()

    for sweep in range(ITERS):
        for d in range(1, tp):
            stat_copy(sweep, d).wait_send()
        for s in range(steps):
            ag_copy(sweep, 0, 0, s).wait_send()
            for g in range(1, groups):
                ag_copy(sweep, 1, g, s).wait_send()
                ag_copy(sweep, 2, g, s).wait_send()
        for g in range(groups):
            part_copy(sweep, g).wait_send()
            if g > 0:
                cross_copy(sweep, g).wait_send()
        pair_copy(sweep).wait_send()
        for c in range(chunks):
            last_copy(sweep, c).wait_send()

        @pl.when(link < pairs - 1)
        def _():
            for c in range(chunks):
                chain_copy(sweep, c).wait_send()


def solution(mesh):
    tm, tp = mesh.shape["tm"], mesh.shape["tp"]
    chunks = 4

    def body(trajectory, offset, step_gaps, qkv_weight, out_weight, mod_weight):
        steps, tok, col = trajectory.shape
        half, rows, groups = col // 2, steps * tok, tp // 2
        table = level_table(5 * steps * tm)
        qkv = jnp.transpose(qkv_weight, (1, 0, 2))
        mod = jnp.transpose(mod_weight, (1, 0, 2))
        anywhere = pl.BlockSpec(memory_space=pl.ANY)
        smem = pl.BlockSpec(memory_space=pltpu.SMEM)
        vm, dma = pltpu.VMEM, pltpu.SemaphoreType.DMA
        return pl.pallas_call(
            functools.partial(kernel, tm, tp, steps, tok, col),
            out_shape=jax.ShapeDtypeStruct(trajectory.shape, F32),
            in_specs=[smem, smem] + [anywhere] * 5,
            out_specs=pl.BlockSpec(memory_space=pltpu.VMEM),
            scratch_shapes=[
                vm(trajectory.shape, F32),
                vm(table.shape, BF16),
                vm(mod.shape, BF16),
                vm(qkv.shape, BF16),
                vm(out_weight.shape, BF16),
                vm((3, 8, col), F32),
                vm((tm, 8, 128), jnp.int32),
                vm((ITERS, tp, 8, rows), F32),
                vm((ITERS, tp, steps, tok, col), BF16),
                vm((3, rows, col), F32),
                vm((rows, col), BF16),
                vm((ITERS, 2, groups, rows, col), BF16),
                vm((ITERS, 2, max(groups - 1, 1), rows, col), BF16),
                vm((steps, tok, col), F32),
                vm((2, tok, half), F32),
                vm((ITERS, tok, half), BF16),
                vm((ITERS, tok, half), BF16),
                vm((ITERS, chunks, tok // chunks, half), BF16),
                vm((ITERS, chunks, tok // chunks, half), BF16),
                vm((ITERS, chunks, tok // chunks, half), BF16),
                vm((ITERS, chunks, tok // chunks, half), BF16),
                vm((2, tok, half), F32),
                vm((tok, col), F32),
                vm((2, tok, col), BF16),
                dma((5,)),
                dma((tm,)),
                dma((tm,)),
                dma((ITERS, 2, tp)),
                dma((ITERS, 2, 3, groups, steps)),
                dma((ITERS, 2, 2, groups)),
                dma((ITERS, 2, 1)),
                dma((ITERS, 4, chunks)),
                dma((tm,)),
                dma,
            ],
            compiler_params=pltpu.CompilerParams(
                collective_id=0, has_side_effects=True, vmem_limit_bytes=62 * 1024 * 1024
            ),
            name="picard",
        )(offset, step_gaps, trajectory, table, mod, qkv, out_weight)

    placed = (
        P("tm", None, "tp"),
        P(),
        P("tm"),
        P(None, None, "tp"),
        P("tp", None),
        P(None, None, "tp"),
    )
    return jax.shard_map(
        body, mesh=mesh, in_specs=placed, out_specs=P("tm", None, "tp"), check_vma=False
    )
```

time: 315 us -> 102 us (0.32)
  waiting for transfers between devices: 197 us -> 0 us
  Pallas kernels: 0 us -> 97.7 us
  matrix products: 34.9 us -> 0 us
  local copies, waits for them, and re-layouts: 29.8 us -> 2.06 us
  other arithmetic: 23.8 us -> 0.96 us
  between operations: 14.4 us -> 0.67 us
  blocking collectives: 7.72 us -> 0 us
  loops' own time: 5.61 us -> 0 us
    all_gather x5 -> x0, waiting for transfers between devices: 140 us -> none  [the longest x2 85.5 us: prefix_2(): gathered = lax.all_gather(array.astype(jnp.bfloat16), axis)]
    pallas_call x0 -> x1, Pallas kernels: none -> 97.7 us  [body(): pl.pallas_call(functools.partial(kernel, tm, tp, steps, tok, col), out_sh...]
    reduce_scatter x2 -> x0, waiting for transfers between devices: 56.3 us -> none  [body(): lax.psum_scatter(head_out.astype(jnp.bfloat16), 'tp', scatter_dimension=2...]
    dot_general x9 -> x0, matrix products: 34 us -> none  [the longest x2 19.1 us: body(): jnp.einsum('std,de->ste', normed, flat_qkv, preferred_element_type=jnp.fl...]
    unnamed x17 -> x1, local copies, waits for them, and re-layouts: 23.4 us -> 2.06 us
    add x16 -> x0, other arithmetic: 13.1 us -> none  [the longest x12 12 us: add_up(): return earlier + later]
    unnamed x1 -> x0, blocking collectives: 7.72 us -> none
    reduce_sum x3 -> x0, other arithmetic: 5.73 us -> none  [the longest x2 5.1 us: body(): row_mean = jnp.sum(whole_rows, -1, keepdims=True) / full_width]
  transfers between devices with their start and end apart: 7 -> 0, of which waited for: 6 -> 0; matrix products, arithmetic and copies ran while one was open for 10% -> 0% of each run, Pallas kernels for 0% -> 0%
where the time goes in v1:
time: 102 us; the launch traced here: 101 us
  Pallas kernels  97.7 us (96%)
  local copies, waits for them, and re-layouts  2.06 us (2%)
    pallas_call x1, Pallas kernels, body(): pl.pallas_call(functools.partial(kernel, tm, tp, steps, tok, col), out_sh...  97.7 us
    unnamed x1, local copies, waits for them, and re-layouts  2.06 us

profile of v1, /device:TPU:24, one launch (start us, length us, event | category | flops | bytes accessed | tf_op | source)
XLA Modules:
  0.0 101.4 jit_solution(14130995325276770711)
XLA Ops:
  0.7 0.3 fusion
  1.0 0.6 pad_maximum_fusion.table_hbm
  1.6 97.7 %picard.1 = f32[2,128,768]{2,1,0:T(8,128)} custom-call(s32[1]{0:T(128)S(6)} %copy.8.offset, s32[2]{0:T(128)} %gaps.1, f32[2,128,768]{2,1,0:T(8,128)} %traj_hbm.1, bf16[128,256]{1,0:T(8,128)(2,1)} %pad_maximum_fusion.table_hbm, bf16[3,256,768]{2,1,0:T(8,128)(2,1)} %bitcast.3, bf16[3,3072,768]{2,1,0:T(8,128)(2,1)} %bitcast.2, bf16[768,3072]{1,0:T(8,128)(2,1)} %out_hbm.1), custom_call_target="tpu_custom_call" | custom-call | tf_op jit(solution)/shard_map/picard/pallas_call | solution.py:376
  99.3 2.1 %copy.9 = f32[2,128,768]{2,1,0:T(8,128)} copy(f32[2,128,768]{2,1,0:T(8,128)} %picard.1) | data formatting | bytes 1572864
  (1 shorter events, 0.0 us)

commit v2 on v1

--- a/solution.py
+++ b/solution.py
@@ -30,16 +30,16 @@
     offset, gaps, traj_hbm, table_hbm, mod_hbm, qkv_hbm, out_hbm, result,
     traj, table, mod_w, qkv_w, out_w, mods,
     gap_buf, stat_buf, normed, acc, attended,
-    rs_part, rs_cross, inc, tot, pair_send, pair_recv, chain_send, chain_recv,
-    last_send, last_recv, prefix, start, start_b,
-    load_sem, gap_send_sem, gap_recv_sem, stat_sem, ag_sem, rs_sem, scan_sem,
+    rs_part, rs_cross, mine, inc, chain_send, chain_recv, last_send,
+    last_recv, prefix, start, start_b,
+    load_sem, gap_send_sem, gap_recv_sem, stat_sem, ag_sem, rs_sem, cross_sem,
     chain_sem, start_send_sem, start_recv_sem,
 ):
     k = lax.axis_index("tm")
     j = lax.axis_index("tp")
     rows = steps * tok
     width = tp * col
-    half = col // 2
+    chunks = chain_send.shape[1]
     groups = tp // 2
     pairs = tm // 2
     core = lax.rem(j, 2)
@@ -142,23 +142,17 @@
             return send(normed.at[sweep, 0, s], normed.at[sweep, 2 * g, s], *sems, k, there)
         return send(normed.at[sweep, 2 * g, s], normed.at[sweep, 2 * g + 1, s], *sems, k, partner)
 
-    def part_copy(sweep, g):
-        return send(
-            rs_part.at[sweep, 0, g], rs_part.at[sweep, 1, g],
-            rs_sem.at[sweep, 0, 0, g], rs_sem.at[sweep, 1, 0, g], k, partner,
-        )
-
-    def cross_copy(sweep, g):
+    def part_copy(sweep, g, s):
+        return send(
+            rs_part.at[sweep, 0, g, s], rs_part.at[sweep, 1, g, s],
+            rs_sem.at[sweep, 0, g, s], rs_sem.at[sweep, 1, g, s], k, partner,
+        )
+
+    def cross_copy(sweep, g, s, c):
         there = lax.rem(group + g, groups) * 2 + core
         return send(
-            rs_cross.at[sweep, 0, g - 1], rs_cross.at[sweep, 1, g - 1],
-            rs_sem.at[sweep, 0, 1, g], rs_sem.at[sweep, 1, 1, g], k, there,
-        )
-
-    def pair_copy(sweep):
-        return send(
-            pair_send.at[sweep], pair_recv.at[sweep],
-            scan_sem.at[sweep, 0, 0], scan_sem.at[sweep, 1, 0], neighbour, j,
+            rs_cross.at[sweep, 0, g - 1, s, c], rs_cross.at[sweep, 1, g - 1, s, c],
+            cross_sem.at[sweep, 0, g, s, c], cross_sem.at[sweep, 1, g, s, c], k, there,
         )
 
     def last_copy(sweep, c):
@@ -173,8 +167,8 @@
             chain_sem.at[sweep, 0, c], chain_sem.at[sweep, 1, c], lax.rem(k + 2, tm), j,
         )
 
-    chunks = chain_send.shape[1]
     piece = tok // chunks
+    last = steps - 1
 
     for sweep in range(ITERS):
         if sweep > 0:
@@ -204,36 +198,23 @@
         if sweep == 0:
             loads[3].wait()
 
-        def project(slot, owner):
-            block = normed[sweep, slot].reshape(rows, col)
+        def project(slot, owner, s=None):
+            block = normed[sweep, slot].reshape(rows, col) if s is None else normed[sweep, slot, s]
+            into = slice(0, rows) if s is None else slice(s * tok, (s + 1) * tok)
             at = pl.multiple_of(owner * col, col)
 
             def one(part, carry):
                 product = jnp.dot(block, qkv_w[part, pl.ds(at, col), :], preferred_element_type=F32)
                 if slot == 0:
-                    acc[part] = product
+                    acc[part, into] = product
                 else:
-                    acc[part] = acc[part] + product
+                    acc[part, into] = acc[part, into] + product
                 return carry
 
             lax.fori_loop(0, 3, one, 0)
 
-        project(0, j)
-        for s in range(steps):
-            ag_copy(sweep, 0, 0, s).wait_recv()
-        project(1, partner)
-        for g in range(1, groups):
-            for s in range(steps):
-                ag_copy(sweep, 1, g, s).wait_recv()
-                ag_copy(sweep, 2, g, s).start()
-            owner = lax.rem(group + groups - g, groups) * 2
-            project(2 * g, owner + core)
-            for s in range(steps):
-                ag_copy(sweep, 2, g, s).wait_recv()
-            project(2 * g + 1, owner + 1 - core)
-
-        def attend(s, carry):
-            at = pl.ds(pl.multiple_of(s * tok, tok), tok)
+        def attend(s):
+            at = slice(s * tok, (s + 1) * tok)
             for head in range(col // HD):
                 lanes = slice(head * HD, (head + 1) * HD)
                 queries = acc[0, at, lanes].astype(BF16)
@@ -244,56 +225,78 @@
                 ) * (1.0 / math.sqrt(HD))
                 weights_exp = jnp.exp(scores - jnp.max(scores, -1, keepdims=True))
                 probs = (weights_exp / jnp.sum(weights_exp, -1, keepdims=True)).astype(BF16)
-                attended[at, lanes] = jnp.dot(
+                attended[s, :, lanes] = jnp.dot(
                     probs, values, preferred_element_type=F32
                 ).astype(BF16)
-            return carry
-
-        lax.fori_loop(0, steps, attend, 0)
-        if sweep == 0:
-            loads[4].wait()
-
-        def head_out(dest):
+
+        def head_out(dest, s):
             at = pl.ds(pl.multiple_of(dest * col, col), col)
-            return jnp.dot(attended[...], out_w[:, at], preferred_element_type=F32)
-
-        for g in list(range(1, groups)) + [0]:
-            there = lax.rem(group + g, groups) * 2
-            rs_part[sweep, 0, g] = head_out(there + 1 - core).astype(BF16)
-            part_copy(sweep, g).start()
-            mine = head_out(there + core)
-            if g > 0:
-                part_copy(sweep, g).wait_recv()
-                rs_cross[sweep, 0, g - 1] = (mine + rs_part[sweep, 1, g].astype(F32)).astype(BF16)
-                cross_copy(sweep, g).start()
-            else:
-                inc[...] = mine.reshape(steps, tok, col)
-        part_copy(sweep, 0).wait_recv()
-        share = inc[...].reshape(rows, col) + rs_part[sweep, 1, 0].astype(F32)
-        for g in range(1, groups):
-            cross_copy(sweep, g).wait_recv()
-            share = share + rs_cross[sweep, 1, g - 1].astype(F32)
-
-        running = jnp.zeros((tok, col), F32)
+            return jnp.dot(attended[s], out_w[:, at], preferred_element_type=F32)
+
+        def pass_on(s):
+            for g in range(1, groups):
+                ag_copy(sweep, 1, g, s).wait_recv()
+                ag_copy(sweep, 2, g, s).start()
+
+        project(0, j)
         for s in range(steps):
-            size = gaps[s].astype(F32) / (5 * steps * tm)
-            running = running - size * (mods[2, s : s + 1] * share[s * tok : (s + 1) * tok])
-            inc[s] = running
-        for h in range(2):
-            tot[h] = running[:, h * half : (h + 1) * half]
-        pair_send[sweep] = tot[1 - side].astype(BF16)
-        pair_copy(sweep).start()
+            ag_copy(sweep, 0, 0, s).wait_recv()
+        project(1, partner)
+        pass_on(0)
+        for s in range(steps):
+            for g in range(1, groups):
+                owner = lax.rem(group + groups - g, groups) * 2
+                project(2 * g, owner + core, s)
+                ag_copy(sweep, 2, g, s).wait_recv()
+                project(2 * g + 1, owner + 1 - core, s)
+            attend(s)
+            if sweep == 0 and s == 0:
+                loads[4].wait()
+            for g in range(1, groups):
+                there = lax.rem(group + g, groups) * 2
+                rs_part[sweep, 0, g, s] = head_out(there + 1 - core, s).astype(BF16)
+                part_copy(sweep, g, s).start()
+                mine[g] = head_out(there + core, s)
+            if s < last:
+                pass_on(s + 1)
+            rs_part[sweep, 0, 0, s] = head_out(partner, s).astype(BF16)
+            part_copy(sweep, 0, s).start()
+            for g in range(1, groups):
+                part_copy(sweep, g, s).wait_recv()
+                for c in range(chunks):
+                    at = slice(c * piece, (c + 1) * piece)
+                    rs_cross[sweep, 0, g - 1, s, c] = (
+                        mine[g, at] + rs_part[sweep, 1, g, s, at].astype(F32)
+                    ).astype(BF16)
+                    cross_copy(sweep, g, s, c).start()
+            inc[s] = head_out(j, s)
+
+        sizes = [gaps[s].astype(F32) / (5 * steps * tm) for s in range(steps)]
+
+        def running(s, c):
+            at = slice(c * piece, (c + 1) * piece)
+            share = inc[s, at] + rs_part[sweep, 1, 0, s, at].astype(F32)
+            for g in range(1, groups):
+                cross_copy(sweep, g, s, c).wait_recv()
+                share = share + rs_cross[sweep, 1, g - 1, s, c].astype(F32)
+            total = -sizes[s] * (mods[2, s : s + 1] * share)
+            if s > 0:
+                total = total + inc[s - 1, at]
+            inc[s, at] = total
+            return total
+
+        for s in range(last):
+            part_copy(sweep, 0, s).wait_recv()
+            for c in range(chunks):
+                running(s, c)
 
         @pl.when(link == 0)
         def _():
             chain_recv[sweep] = jnp.zeros_like(chain_recv[sweep])
 
-        pair_copy(sweep).wait_recv()
-        first = side == 0
+        part_copy(sweep, 0, last).wait_recv()
         for c in range(chunks):
-            at = slice(c * piece, (c + 1) * piece)
-            ours = tot[side, at]
-            theirs = pair_recv[sweep, at].astype(F32)
+            ours = running(last, c)
 
             @pl.when(link > 0)
             def _():
@@ -303,12 +306,12 @@
 
             @pl.when(link < pairs - 1)
             def _():
-                chain_send[sweep, c] = (earlier + ours + theirs).astype(BF16)
+                chain_send[sweep, c] = (earlier + ours).astype(BF16)
                 chain_copy(sweep, c).start()
 
-            last_send[sweep, c] = jnp.where(first, earlier + ours, earlier).astype(BF16)
+            last_send[sweep, c] = jnp.where(side == 0, earlier + ours, earlier).astype(BF16)
             last_copy(sweep, c).start()
-            prefix[side, at] = jnp.where(first, earlier, earlier + theirs)
+            prefix[c] = earlier
         if sweep == 0:
             @pl.when(k > 0)
             def _():
@@ -319,16 +322,16 @@
             def _():
                 start[...] = traj[0]
         for c in range(chunks):
+            at = slice(c * piece, (c + 1) * piece)
             last_copy(sweep, c).wait_recv()
-            prefix[1 - side, c * piece : (c + 1) * piece] = last_recv[sweep, c].astype(F32)
-        entry = start[...] + jnp.concatenate([prefix[0], prefix[1]], -1)
-        if sweep < ITERS - 1:
-            traj[0] = entry
-            for s in range(1, steps):
-                traj[s] = entry + inc[s - 1]
-        else:
-            for s in range(steps):
-                result[s] = entry + inc[s]
+            entry = start[at] + (prefix[c] + last_recv[sweep, c].astype(F32))
+            if sweep < ITERS - 1:
+                traj[0, at] = entry
+                for s in range(1, steps):
+                    traj[s, at] = entry + inc[s - 1, at]
+            else:
+                for s in range(steps):
+                    result[s, at] = entry + inc[s, at]
 
     for d in range(1, tm):
         gap_copy(d).wait_send()
@@ -346,11 +349,10 @@
             for g in range(1, groups):
                 ag_copy(sweep, 1, g, s).wait_send()
                 ag_copy(sweep, 2, g, s).wait_send()
-        for g in range(groups):
-            part_copy(sweep, g).wait_send()
-            if g > 0:
-                cross_copy(sweep, g).wait_send()
-        pair_copy(sweep).wait_send()
+            for g in range(groups):
+                part_copy(sweep, g, s).wait_send()
+                for c in range(chunks if g > 0 else 0):
+                    cross_copy(sweep, g, s, c).wait_send()
         for c in range(chunks):
             last_copy(sweep, c).wait_send()
 
@@ -362,11 +364,12 @@
 
 def solution(mesh):
     tm, tp = mesh.shape["tm"], mesh.shape["tp"]
-    chunks = 4
+    chunks = 8
 
     def body(trajectory, offset, step_gaps, qkv_weight, out_weight, mod_weight):
         steps, tok, col = trajectory.shape
-        half, rows, groups = col // 2, steps * tok, tp // 2
+        rows, groups = steps * tok, tp // 2
+        pieces = (chunks, tok // chunks, col)
         table = level_table(5 * steps * tm)
         qkv = jnp.transpose(qkv_weight, (1, 0, 2))
         mod = jnp.transpose(mod_weight, (1, 0, 2))
@@ -389,18 +392,16 @@
                 vm((ITERS, tp, 8, rows), F32),
                 vm((ITERS, tp, steps, tok, col), BF16),
                 vm((3, rows, col), F32),
-                vm((rows, col), BF16),
-                vm((ITERS, 2, groups, rows, col), BF16),
-                vm((ITERS, 2, max(groups - 1, 1), rows, col), BF16),
+                vm((steps, tok, col), BF16),
+                vm((ITERS, 2, groups, steps, tok, col), BF16),
+                vm((ITERS, 2, max(groups - 1, 1), steps) + pieces, BF16),
+                vm((groups, tok, col), F32),
                 vm((steps, tok, col), F32),
-                vm((2, tok, half), F32),
-                vm((ITERS, tok, half), BF16),
-                vm((ITERS, tok, half), BF16),
-                vm((ITERS, chunks, tok // chunks, half), BF16),
-                vm((ITERS, chunks, tok // chunks, half), BF16),
-                vm((ITERS, chunks, tok // chunks, half), BF16),
-                vm((ITERS, chunks, tok // chunks, half), BF16),
-                vm((2, tok, half), F32),
+                vm((ITERS,) + pieces, BF16),
+                vm((ITERS,) + pieces, BF16),
+                vm((ITERS,) + pieces, BF16),
+                vm((ITERS,) + pieces, BF16),
+                vm(pieces, F32),
                 vm((tok, col), F32),
                 vm((2, tok, col), BF16),
                 dma((5,)),
@@ -408,8 +409,8 @@
                 dma((tm,)),
                 dma((ITERS, 2, tp)),
                 dma((ITERS, 2, 3, groups, steps)),
-                dma((ITERS, 2, 2, groups)),
-                dma((ITERS, 2, 1)),
+                dma((ITERS, 2, groups, steps)),
+                dma((ITERS, 2, groups, steps, chunks)),
                 dma((ITERS, 4, chunks)),
                 dma((tm,)),
                 dma,

time: 102 us -> 82.3 us (0.81)
  Pallas kernels: 97.7 us -> 78.4 us
    pallas_call x1, Pallas kernels: 97.7 us -> 78.4 us  [body(): pl.pallas_call(functools.partial(kernel, tm, tp, steps, tok, col), out_sh...]
where the time goes in v2:
time: 82.3 us; the launch traced here: 82.1 us
  Pallas kernels  78.4 us (95%)
  local copies, waits for them, and re-layouts  2.06 us (3%)
  other arithmetic  0.96 us (1%)
    pallas_call x1, Pallas kernels, body(): pl.pallas_call(functools.partial(kernel, tm, tp, steps, tok, col), out_sh...  78.4 us
    unnamed x1, local copies, waits for them, and re-layouts  2.06 us

profile of v2, /device:TPU:24, one launch (start us, length us, event | category | flops | bytes accessed | tf_op | source)
XLA Modules:
  0.0 82.1 jit_solution(6784084877931536176)
XLA Ops:
  0.7 0.3 fusion
  1.0 0.6 pad_maximum_fusion.table_hbm
  1.6 78.4 %picard.1 = f32[2,128,768]{2,1,0:T(8,128)} custom-call(s32[1]{0:T(128)S(6)} %copy.8.offset, s32[2]{0:T(128)} %gaps.1, f32[2,128,768]{2,1,0:T(8,128)} %traj_hbm.1, bf16[128,256]{1,0:T(8,128)(2,1)} %pad_maximum_fusion.table_hbm, bf16[3,256,768]{2,1,0:T(8,128)(2,1)} %bitcast.3, bf16[3,3072,768]{2,1,0:T(8,128)(2,1)} %bitcast.2, bf16[768,3072]{1,0:T(8,128)(2,1)} %out_hbm.1), custom_call_target="tpu_custom_call" | custom-call | tf_op jit(solution)/shard_map/picard/pallas_call | solution.py:379
  80.0 2.1 %copy.9 = f32[2,128,768]{2,1,0:T(8,128)} copy(f32[2,128,768]{2,1,0:T(8,128)} %picard.1) | data formatting | bytes 1572864
  (1 shorter events, 0.0 us)

commit v3 on v2

--- a/solution.py
+++ b/solution.py
@@ -27,13 +27,13 @@
 
 def kernel(
     tm, tp, steps, tok, col,
-    offset, gaps, traj_hbm, table_hbm, mod_hbm, qkv_hbm, out_hbm, result,
+    offset, gaps, traj_hbm, table_hbm, mod_hbm, qkv_hbm, out_hbm, entry_out, inc_out,
     traj, table, mod_w, qkv_w, out_w, mods,
     gap_buf, stat_buf, normed, acc, attended,
     rs_part, rs_cross, mine, inc, chain_send, chain_recv, last_send,
     last_recv, prefix, start, start_b,
     load_sem, gap_send_sem, gap_recv_sem, stat_sem, ag_sem, rs_sem, cross_sem,
-    chain_sem, start_send_sem, start_recv_sem,
+    chain_sem, start_send_sem, start_recv_sem, inc_sem, sums,
 ):
     k = lax.axis_index("tm")
     j = lax.axis_index("tp")
@@ -55,7 +55,7 @@
             ((traj_hbm, traj), (table_hbm, table), (mod_hbm, mod_w), (qkv_hbm, qkv_w), (out_hbm, out_w))
         )
     ]
-    for load in loads:
+    for load in loads[:3]:
         load.start()
 
     barrier = pltpu.get_barrier_semaphore()
@@ -79,16 +79,22 @@
         own_total = own_total + gaps[s]
     gap_buf[0] = jnp.full((8, 128), own_total, jnp.int32)
     loads[0].wait()
-
-    def stats_of(sweep):
-        x = traj[...].reshape(rows, col)
+    for load in loads[3:]:
+        load.start()
+
+    def row_sums(s, at):
+        x = traj[s, at]
         total = jnp.sum(x, -1, keepdims=True)
         squares = jnp.sum(x * x, -1, keepdims=True)
-        lane = lax.broadcasted_iota(jnp.int32, (rows, 128), 1)
-        both = jnp.where(lane == 0, total, jnp.where(lane == 1, squares, 0.0))
-        stat_buf[sweep, 0] = jnp.transpose(both)[0:8]
-
-    stats_of(0)
+        lane = lax.broadcasted_iota(jnp.int32, (x.shape[0], 128), 1)
+        sums[s, at] = jnp.where(lane == 0, total, jnp.where(lane == 1, squares, 0.0))
+
+    def turn_sums(sweep):
+        stat_buf[sweep, 0] = jnp.transpose(sums[...].reshape(rows, 128))[0:8]
+
+    for s in range(steps):
+        row_sums(s, slice(0, tok))
+    turn_sums(0)
     start_b[0] = traj[0].astype(BF16)
     pl.semaphore_wait(barrier, tp - 1 + tm - 1)
 
@@ -167,12 +173,15 @@
             chain_sem.at[sweep, 0, c], chain_sem.at[sweep, 1, c], lax.rem(k + 2, tm), j,
         )
 
+    def inc_copy(n):
+        return pltpu.make_async_copy(inc.at[n], inc_out.at[n], inc_sem.at[n])
+
     piece = tok // chunks
     last = steps - 1
 
     for sweep in range(ITERS):
         if sweep > 0:
-            stats_of(sweep)
+            turn_sums(sweep)
             for d in range(1, tp):
                 stat_copy(sweep, d).start()
         stats = stat_buf[sweep, 0]
@@ -215,18 +224,23 @@
 
         def attend(s):
             at = slice(s * tok, (s + 1) * tok)
-            for head in range(col // HD):
-                lanes = slice(head * HD, (head + 1) * HD)
-                queries = acc[0, at, lanes].astype(BF16)
-                key_rows = acc[1, at, lanes].astype(BF16)
-                values = acc[2, at, lanes].astype(BF16)
-                scores = lax.dot_general(
-                    queries, key_rows, (((1,), (1,)), ((), ())), preferred_element_type=F32
-                ) * (1.0 / math.sqrt(HD))
-                weights_exp = jnp.exp(scores - jnp.max(scores, -1, keepdims=True))
-                probs = (weights_exp / jnp.sum(weights_exp, -1, keepdims=True)).astype(BF16)
+            heads = [slice(head * HD, (head + 1) * HD) for head in range(col // HD)]
+            scores = jnp.concatenate(
+                [
+                    lax.dot_general(
+                        acc[0, at, lanes].astype(BF16), acc[1, at, lanes].astype(BF16),
+                        (((1,), (1,)), ((), ())), preferred_element_type=F32,
+                    )
+                    for lanes in heads
+                ],
+                0,
+            ) * (1.0 / math.sqrt(HD))
+            weights_exp = jnp.exp(scores - jnp.max(scores, -1, keepdims=True))
+            probs = (weights_exp / jnp.sum(weights_exp, -1, keepdims=True)).astype(BF16)
+            for head, lanes in enumerate(heads):
                 attended[s, :, lanes] = jnp.dot(
-                    probs, values, preferred_element_type=F32
+                    probs[head * tok : (head + 1) * tok], acc[2, at, lanes].astype(BF16),
+                    preferred_element_type=F32,
                 ).astype(BF16)
 
         def head_out(dest, s):
@@ -312,6 +326,9 @@
             last_send[sweep, c] = jnp.where(side == 0, earlier + ours, earlier).astype(BF16)
             last_copy(sweep, c).start()
             prefix[c] = earlier
+        if sweep == ITERS - 1:
+            for n in range(steps):
+                inc_copy(n).start()
         if sweep == 0:
             @pl.when(k > 0)
             def _():
@@ -329,10 +346,13 @@
                 traj[0, at] = entry
                 for s in range(1, steps):
                     traj[s, at] = entry + inc[s - 1, at]
+                for s in range(steps):
+                    row_sums(s, at)
             else:
-                for s in range(steps):
-                    result[s, at] = entry + inc[s, at]
-
+                entry_out[at] = entry
+
+    for n in range(steps):
+        inc_copy(n).wait()
     for d in range(1, tm):
         gap_copy(d).wait_send()
 
@@ -376,11 +396,14 @@
         anywhere = pl.BlockSpec(memory_space=pl.ANY)
         smem = pl.BlockSpec(memory_space=pltpu.SMEM)
         vm, dma = pltpu.VMEM, pltpu.SemaphoreType.DMA
-        return pl.pallas_call(
+        entry, increments = pl.pallas_call(
             functools.partial(kernel, tm, tp, steps, tok, col),
-            out_shape=jax.ShapeDtypeStruct(trajectory.shape, F32),
+            out_shape=(
+                jax.ShapeDtypeStruct((tok, col), F32),
+                jax.ShapeDtypeStruct(trajectory.shape, F32),
+            ),
             in_specs=[smem, smem] + [anywhere] * 5,
-            out_specs=pl.BlockSpec(memory_space=pltpu.VMEM),
+            out_specs=(pl.BlockSpec(memory_space=pltpu.VMEM), anywhere),
             scratch_shapes=[
                 vm(trajectory.shape, F32),
                 vm(table.shape, BF16),
@@ -414,12 +437,15 @@
                 dma((ITERS, 4, chunks)),
                 dma((tm,)),
                 dma,
+                dma((steps,)),
+                vm((steps, tok, 128), F32),
             ],
             compiler_params=pltpu.CompilerParams(
                 collective_id=0, has_side_effects=True, vmem_limit_bytes=62 * 1024 * 1024
             ),
             name="picard",
         )(offset, step_gaps, trajectory, table, mod, qkv, out_weight)
+        return entry[None] + increments
 
     placed = (
         P("tm", None, "tp"),

time: 82.3 us -> 79.4 us (0.965)
  Pallas kernels: 78.4 us -> 75.4 us
  other arithmetic: 0.96 us -> 3.15 us
  local copies, waits for them, and re-layouts: 2.06 us -> 0 us
    pallas_call x1, Pallas kernels: 78.4 us -> 75.4 us  [body(): pl.pallas_call(functools.partial(kernel, tm, tp, steps, tok, col), out_sh...]
    add x0 -> x1, other arithmetic: none -> 2.18 us  [body(): return entry[None] + increments]
    unnamed x1 -> x0, local copies, waits for them, and re-layouts: 2.06 us -> none
where the time goes in v3:
time: 79.4 us; the launch traced here: 79.2 us
  Pallas kernels  75.4 us (95%)
  other arithmetic  3.15 us (4%)
    pallas_call x1, Pallas kernels, body(): pl.pallas_call(functools.partial(kernel, tm, tp, steps, tok, col), out_sh...  75.4 us
    add x1, other arithmetic, body(): return entry[None] + increments  2.18 us

profile of v3, /device:TPU:24, one launch (start us, length us, event | category | flops | bytes accessed | tf_op | source)
XLA Modules:
  0.0 79.2 jit_solution(3672539171220966536)
XLA Ops:
  0.7 0.3 fusion
  1.0 0.6 pad_maximum_fusion.table_hbm
  1.6 75.4 %picard.1 = (f32[128,768]{1,0:T(8,128)}, f32[2,128,768]{2,1,0:T(8,128)}) custom-call(s32[1]{0:T(128)S(6)} %copy.7.offset, s32[2]{0:T(128)} %gaps.1, f32[2,128,768]{2,1,0:T(8,128)} %traj_hbm.1, bf16[128,256]{1,0:T(8,128)(2,1)} %pad_maximum_fusion.table_hbm, bf16[3,256,768]{2,1,0:T(8,128)(2,1)} %bitcast.3, bf16[3,3072,768]{2,1,0:T(8,128)(2,1)} %bitcast.2, ...), custom_call_target="tpu_custom_call" | custom-call | tf_op jit(solution)/shard_map/picard/pallas_call | solution.py:399
  77.0 2.2 %broadcast_add_fusion = f32[2,128,768]{2,1,0:T(8,128)} fusion(f32[2,128,768]{2,1,0:T(8,128)} %get-tuple-element.8, f32[128,768]{1,0:T(8,128)} %get-tuple-element.7), kind=kLoop, calls=%fused_computation | loop fusion | flops 196608 | bytes 1966080 | tf_op jit(solution)/shard_map/add | solution.py:448
  (1 shorter events, 0.0 us)

commit v4 on v3

--- a/solution.py
+++ b/solution.py
@@ -441,7 +441,7 @@
                 vm((steps, tok, 128), F32),
             ],
             compiler_params=pltpu.CompilerParams(
-                collective_id=0, has_side_effects=True, vmem_limit_bytes=62 * 1024 * 1024
+                collective_id=0, has_side_effects=True, vmem_limit_bytes=51 * 1024 * 1024
             ),
             name="picard",
         )(offset, step_gaps, trajectory, table, mod, qkv, out_weight)

time: 79.4 us -> 78.6 us (0.990)
  other arithmetic: 3.15 us -> 1.28 us
  local copies, waits for them, and re-layouts: 0 us -> 1.78 us
    unnamed x0 -> x4, local copies, waits for them, and re-layouts: none -> 1.78 us
    add x1, other arithmetic: 2.18 us -> 0.95 us  [body(): return entry[None] + increments]
where the time goes in v4:
time: 78.6 us; the launch traced here: 78.4 us
  Pallas kernels  74.7 us (95%)
  local copies, waits for them, and re-layouts  1.78 us (2%)
  other arithmetic  1.28 us (2%)
    pallas_call x1, Pallas kernels, body(): pl.pallas_call(functools.partial(kernel, tm, tp, steps, tok, col), out_sh...  74.7 us
    unnamed x4, local copies, waits for them, and re-layouts  1.78 us

profile of v4, /device:TPU:24, one launch (start us, length us, event | category | flops | bytes accessed | tf_op | source)
XLA Modules:
  0.0 78.4 jit_solution(12094916375586912240)
XLA Ops:
  0.7 0.3 fusion
  1.0 0.0 copy-start
  1.0 1.1 %copy-done = f32[2,128,768]{2,1,0:T(8,128)S(1)} copy-done((f32[2,128,768]{2,1,0:T(8,128)S(1)}, f32[2,128,768]{2,1,0:T(8,128)}, u32[]{:S(2)}) %copy-start) | copy-done | bytes 786456
  2.1 0.0 copy-start.1
  2.1 0.7 copy-done.1
  2.8 74.7 %picard.1 = (f32[128,768]{1,0:T(8,128)S(1)}, f32[2,128,768]{2,1,0:T(8,128)S(1)}) custom-call(s32[1]{0:T(128)S(6)} %copy.7.offset, s32[2]{0:T(128)S(1)} %copy-done.1, f32[2,128,768]{2,1,0:T(8,128)S(1)} %copy-done, bf16[128,256]{1,0:T(8,128)(2,1)S(1)} %pad_maximum_fusion.table_hbm, bf16[3,256,768]{2,1,0:T(8,128)(2,1)} %bitcast.3, ...), custom_call_target="tpu_custom_call" | custom-call | tf_op jit(solution)/shard_map/picard/pallas_call | solution.py:399
  77.5 0.9 %broadcast_add_fusion = f32[2,128,768]{2,1,0:T(8,128)} fusion(f32[2,128,768]{2,1,0:T(8,128)S(1)} %get-tuple-element.8, f32[128,768]{1,0:T(8,128)S(1)} %get-tuple-element.7), kind=kLoop, calls=%fused_computation | loop fusion | flops 196608 | bytes 1966080 | tf_op jit(solution)/shard_map/add | solution.py:448
  (2 shorter events, 0.0 us)
Async XLA Ops:
  1.0 1.1 %copy-start = (f32[2,128,768]{2,1,0:T(8,128)S(1)}, f32[2,128,768]{2,1,0:T(8,128)}, u32[]{:S(2)}) copy-start(f32[2,128,768]{2,1,0:T(8,128)} %traj_hbm.1) | copy-start | bytes 2359300
  2.1 0.7 copy-start.1
